TPU v7x, 16 devices: a whole 2x2x2 slice. The times are simulated.
16 devices in a mesh: dp: 1, sp: 16 (over x, y, z, core).
Axes of the slice: x: 2, y: 2, z: 2, core: 2. Of those that a mesh axis runs over, the one named last changes fastest.
Arguments:
- q: bfloat16 [32, 56, 128], P('dp')
- k: bfloat16 [32, 4096, 56, 128], P('dp', 'sp')
- v: bfloat16 [32, 4096, 56, 128], P('dp', 'sp')
Outputs:
- q: bfloat16 [32, 56, 128], P('dp')
All inputs are finite; a program needn't handle non-finite values.
Results may differ from a plain program's by a relative error of at most 0.012.
Values are sent between devices in bfloat16 or wider.
A program may use at most 2 GiB of HBM per device.

v0:
```python
import jax
import jax.numpy as jnp
from jax import lax
from jax.sharding import PartitionSpec as P


def einsum(form, a, b):
    return jnp.einsum(form, a.astype(jnp.float32), b.astype(jnp.float32))


def part_of(q, k, v):
    grouped = q.reshape(q.shape[0], k.shape[2], -1, q.shape[2])
    scores = einsum("bgsd,bugd->bgsu", grouped, k) * q.shape[2] ** -0.5
    high = jnp.max(scores, -1, keepdims=True)
    weights = jnp.exp(scores - high)
    seen = einsum("bgsu,bugd->bgsd", weights.astype(jnp.bfloat16), v)
    return jnp.concatenate([seen, jnp.sum(weights, -1, keepdims=True), high], -1)


def together(parts):
    seen, total, high = parts[..., :-2], parts[..., -2:-1], parts[..., -1:]
    scale = jnp.exp(high - jnp.max(high, 0))
    return (jnp.sum(seen * scale, 0) / jnp.sum(total * scale, 0)).astype(jnp.bfloat16)


def solution(mesh):
    def step(q, k, v):
        return together(lax.all_gather(part_of(q, k, v), "sp")).reshape(q.shape)

    return jax.shard_map(
        step,
        mesh=mesh,
        in_specs=(P("dp", None, None), P("dp", "sp", None, None), P("dp", "sp", None, None)),
        out_specs=P("dp", None, None),
        check_vma=False,
    )
```

profile of v0, /device:TPU:0, one launch (start us, length us, event | category | flops | bytes accessed | tf_op | source)
XLA Modules:
  0.0 268.7 jit_solution(8466371404573908696)
XLA Ops:
  6.5 0.0 all-gather.3.cloned.1.call-start
  6.5 42.6 %fusion.2 = f32[32,56,1,256]{3,2,1,0:T(1,128)S(1)} fusion(bf16[32,256,56,128]{3,2,1,0:T(8,128)(2,1)} %param.4, bf16[32,56,128,1]{2,1,0,3:T(8,128)(2,1)} %bitcast.22), kind=kOutput, calls=%fused_computation.2 | convolution fusion | flops 117440512 | bytes 119734272 | tf_op jit(solution)/shard_map/bgsd,bugd->bgsu/dot_general | solution.py:8
  49.1 0.3 fusion.8
  49.4 0.7 fusion.9
  50.1 42.4 %fusion = f32[32,56,1,128]{3,2,1,0:T(1,128)S(1)} fusion(bf16[32,256,56,128]{3,2,1,0:T(8,128)(2,1)} %param.5, bf16[32,56,256,1]{2,1,0,3:T(8,128)(2,1)S(1)} %get-tuple-element.7), kind=kOutput, calls=%fused_computation | convolution fusion | flops 117440512 | bytes 119275520 | tf_op jit(solution)/shard_map/bgsu,bugd->bgsd/dot_general | solution.py:8
  92.5 1.2 copy.12
  93.7 1.6 pad_maximum_fusion
  95.3 0.0 all-gather.3.cloned.1.call-update
  95.3 148.3 %all-gather.3.cloned.1.call-done = f32[512,56,1,130]{1,0,3,2:T(8,128)} async-done(((f32[32,56,1,130]{1,0,3,2:T(8,128)}), f32[512,56,1,130]{1,0,3,2:T(8,128)}) %all-gather.3.cloned.1.call-update) | async-done | bytes 14909456 | tf_op jit(solution)/shard_map/all_gather | solution.py:28
  243.6 1.0 slice_reduce_fusion
  244.5 1.1 fusion.11
  245.6 14.1 %fusion.4 = f32[32,56,128]{1,0,2:T(8,128)S(1)} fusion(f32[16,32,56,1,130]{2,1,0,4,3:T(8,128)} %bitcast.21, f32[16,32,56]{2,1,0:T(8,128)S(1)} %get-tuple-element.6), kind=kLoop, calls=%fused_computation.5 | loop fusion | flops 7110656 | bytes 15712256 | tf_op jit(solution)/shard_map/reduce_sum | solution.py:23
  259.8 0.2 divide_convert_fusion
  260.0 1.8 copy.6
Async XLA Ops:
  6.5 237.0 %all-gather.3.cloned.1.call-start = ((), (), s32[]{:S(2)}) async-start(), calls=%async_computation | async-start | bytes 36208640 | tf_op jit(solution)/shard_map/all_gather | solution.py:28
Sparse Core Ops, SparseCore 0:
  95.4 148.1 all-gather.2
where the time goes:
time: 269 us
  waiting for transfers between devices  148 us (55%)
  matrix products  85 us (32%)
  other arithmetic  19 us (7%)
  between operations  13.4 us (5%)
  local copies, waits for them, and re-layouts  3.02 us (1%)
    all_gather x1, waiting for transfers between devices, step(): return together(lax.all_gather(part_of(q, k, v), 'sp')).reshape(q.shape)  148 us
    dot_general x2, matrix products, einsum(): return jnp.einsum(form, a.astype(jnp.float32), b.astype(jnp.float32))  85 us
    reduce_sum x1, other arithmetic, together(): jnp.sum(seen * scale, 0) / jnp.sum(total * scale, 0)  14.1 us
  transfers between devices with their start and end apart: 1, of which 1 were waited for; matrix products, arithmetic and copies ran while one was open for 0% of the time, Pallas kernels for 0%

commit v1 on v0

v1 whole, which is shorter than its diff:
```python
import functools

import jax
import jax.numpy as jnp
from jax import lax
from jax.experimental import pallas as pl
from jax.experimental.pallas import tpu as pltpu
from jax.sharding import PartitionSpec as P

F32, BF16 = jnp.float32, jnp.bfloat16
LOG2E = 1.4426950408889634
CHUNK = 32
SLOTS = 4
LAST = 2
DELAY = 4
LANES = 128


def kernel(n, scale, q_hbm, k_hbm, v_hbm, out, q, keys, values, mask, scores, high, part, stats, parts, allstats, in_sem, sums_sem, sumr_sem, res_sems, res_semr, all_sems):
    count, heads, head = out.shape
    rows = keys.shape[1]
    chunk = CHUNK * heads
    owned = pl.cdiv(count, n)
    early = count - LAST
    me = lax.axis_index("sp")

    def fetch(i, which):
        slot = lax.rem(i, SLOTS)
        cache, here = ((k_hbm, keys), (v_hbm, values))[which]
        return pltpu.make_async_copy(cache.at[pl.ds(i * rows, rows)], here.at[slot], in_sem.at[which, slot])

    q_copy = pltpu.make_async_copy(q_hbm, q, in_sem.at[2, 0])
    q_copy.start()
    fetch(0, 0).start()
    for i in range(1, SLOTS):
        fetch(i, 0).start()
        fetch(i - 1, 1).start()
    fetch(SLOTS - 1, 1).start()

    barrier = pltpu.get_barrier_semaphore()
    for step in range(1, n):
        pl.semaphore_signal(barrier, inc=1, device_id={"sp": lax.rem(me + step, n)})

    column = lax.broadcasted_iota(jnp.int32, (heads, chunk), 1).astype(F32)
    column = column - heads * jnp.floor((column + 0.5) * (1 / heads))
    row = lax.broadcasted_iota(jnp.int32, (heads, chunk), 0).astype(F32)
    mask[...] = jnp.where(column == row, jnp.inf, -jnp.inf)

    lane = lax.broadcasted_iota(jnp.int32, (heads, LANES), 1)
    line = lax.broadcasted_iota(jnp.int32, (heads, LANES), 0)
    own_lane = lane == line

    def score(i):
        slot = lax.rem(i, SLOTS)
        best = []

        def one(j):
            got = lax.dot_general(q[i], keys[slot, pl.ds(j * chunk, chunk), :], (((1,), (1,)), ((), ())), preferred_element_type=F32)
            got = jnp.minimum(got, mask[...])
            scores[:, pl.ds(j * chunk, chunk)] = got
            for g in range(chunk // LANES):
                piece = got[:, g * LANES : (g + 1) * LANES]
                best[:] = [jnp.maximum(best[0], piece) if best else piece]

        def end():
            high[...] = jnp.broadcast_to(jnp.max(best[0], -1, keepdims=True), (heads, LANES))

        return one, end

    def value(i):
        slot = lax.rem(i, SLOTS)
        top = high[...]
        total, seen = [], []

        def one(j):
            weights = []
            for g in range(chunk // LANES):
                w = jnp.exp2((scores[:, pl.ds(j * chunk + g * LANES, LANES)] - top) * (scale * LOG2E))
                total[:] = [total[0] + w if total else w]
                weights.append(w.astype(BF16))
            got = jnp.dot(jnp.concatenate(weights, 1), values[slot, pl.ds(j * chunk, chunk), :], preferred_element_type=F32)
            seen[:] = [seen[0] + got if seen else got]

        def end():
            sums = jnp.sum(total[0], -1, keepdims=True)
            part[i] = seen[0].astype(BF16)
            both = jnp.where(own_lane, top, 0.0) + jnp.where(lane == line + LANES // 2, sums, 0.0)
            stats[i] = jnp.sum(both, 0, keepdims=True)

        return one, end

    def part_copies(i, place, there, sems, semr):
        return [
            pltpu.make_async_remote_copy(part.at[i], parts.at[place, me], sems[0], semr[0], device_id={"sp": there}),
            pltpu.make_async_remote_copy(stats.at[i], allstats.at[place, me], sems[1], semr[1], device_id={"sp": there}),
        ]

    def to_owner(i):
        place = i // n
        return part_copies(
            i, place, lax.rem(i, n), (sums_sem.at[0, i], sums_sem.at[1, i]), (sumr_sem.at[0, place, me], sumr_sem.at[1, place, me])
        )

    def keep(i, place):
        parts[place, me] = part[i]
        allstats[place, me] = stats[i]

    def other(flips):
        there = me
        for bit in range(4):
            if flips >> bit & 1:
                there = there + (1 - 2 * lax.rem(me // 2**bit, 2)) * 2**bit
        return there

    order = sorted(range(1, n), key=lambda flips: (-bin(flips >> 1).count("1"), flips))

    def to_all(i, flips):
        which = i - early
        place = owned + which
        there = other(flips)
        return part_copies(
            i,
            place,
            there,
            (all_sems.at[0, which, flips], all_sems.at[1, which, flips]),
            (sumr_sem.at[0, place, me], sumr_sem.at[1, place, me]),
        )

    def arrived(place):
        for flips in order:
            there = other(flips)
            pltpu.make_async_copy(parts.at[place, there], parts.at[place, there], sumr_sem.at[0, place, there]).wait()
            pltpu.make_async_copy(allstats.at[place, there], allstats.at[place, there], sumr_sem.at[1, place, there]).wait()

    def combine(place, i):
        both = jnp.concatenate([allstats[place, s] for s in range(n)], 0)
        sums = pltpu.roll(both, LANES // 2, 1)
        share = jnp.exp2((both - jnp.max(both, 0, keepdims=True)) * (scale * LOG2E))
        share = share / jnp.sum(share * sums, 0, keepdims=True)
        got = None
        for s in range(n):
            mine = jnp.broadcast_to(share[s : s + 1], (heads, LANES))
            mine = jnp.sum(jnp.where(own_lane, mine, 0.0), -1, keepdims=True)
            term = mine * parts[place, s].astype(F32)
            got = term if got is None else got + term
        out[i] = got.astype(BF16)

    def result_copy(i, there, slot):
        return pltpu.make_async_remote_copy(
            out.at[i], out.at[i], res_sems.at[i // n, slot], res_semr.at[i], device_id={"sp": there}
        )

    def finish(i):
        @pl.when(lax.rem(i, n) == me)
        def _():
            place = i // n
            arrived(place)
            combine(place, i)
            for flips in order:
                result_copy(i, other(flips), flips).start()

    q_copy.wait()
    fetch(0, 0).wait()
    one, end = score(0)
    for j in range(rows // chunk):
        one(j)
    end()
    pl.semaphore_wait(barrier, n - 1)

    def step(i, _):
        @pl.when(jnp.logical_and(i >= 2, i + SLOTS - 2 < count))
        def _():
            fetch(i + SLOTS - 2, 1).start()

        @pl.when(i + SLOTS - 1 < count)
        def _():
            fetch(i + SLOTS - 1, 0).start()

        fetch(i, 0).wait()
        fetch(i - 1, 1).wait()
        value_one, value_end = value(i - 1)
        score_one, score_end = score(i)
        for j in range(rows // chunk):
            value_one(j)
            score_one(j)
        value_end()
        score_end()

        last = i - 1

        @pl.when(jnp.logical_and(last < early, lax.rem(last, n) != me))
        def _():
            for copy in to_owner(last):
                copy.start()

        @pl.when(jnp.logical_and(last < early, lax.rem(last, n) == me))
        def _():
            keep(last, last // n)

        for i_all in range(early, count - 1):

            @pl.when(last == i_all)
            def _():
                for flips in order:
                    for copy in to_all(i_all, flips):
                        copy.start()
                keep(i_all, owned + i_all - early)

        @pl.when(last >= DELAY)
        def _():
            finish(last - DELAY)

        return 0

    lax.fori_loop(1, count, step, 0)

    end_i = count - 1
    fetch(end_i, 1).wait()
    one, end = value(end_i)
    for j in range(rows // chunk):
        one(j)
    end()
    for flips in order:
        for copy in to_all(end_i, flips):
            copy.start()
    keep(end_i, owned + LAST - 1)

    for i in range(count - 1 - DELAY, early):
        finish(i)
    for i in range(early, count):
        arrived(owned + i - early)
        combine(owned + i - early, i)

    def ends(i, _):
        @pl.when(lax.rem(i, n) != me)
        def _():
            for copy in to_owner(i):
                copy.wait_send()
            result_copy(i, 0, 0).wait_recv()

        @pl.when(lax.rem(i, n) == me)
        def _():
            for flips in order:
                result_copy(i, other(flips), flips).wait_send()

        return 0

    lax.fori_loop(0, early, ends, 0)
    for i in range(early, count):
        for flips in order:
            for copy in to_all(i, flips):
                copy.wait_send()


def solution(mesh):
    n = mesh.shape["sp"]

    def step(q, k, v):
        count, tokens, heads, head = k.shape
        rows = tokens * heads
        owned = pl.cdiv(count, n)
        places = owned + LAST
        anywhere = pl.BlockSpec(memory_space=pl.ANY)
        dma = pltpu.SemaphoreType.DMA
        return pl.pallas_call(
            functools.partial(kernel, n, head**-0.5),
            out_shape=jax.ShapeDtypeStruct(q.shape, BF16),
            in_specs=[anywhere] * 3,
            out_specs=pl.BlockSpec(memory_space=pltpu.VMEM),
            scratch_shapes=[
                pltpu.VMEM(q.shape, BF16),
                pltpu.VMEM((SLOTS, rows, head), BF16),
                pltpu.VMEM((SLOTS, rows, head), BF16),
                pltpu.VMEM((heads, CHUNK * heads), F32),
                pltpu.VMEM((heads, rows), F32),
                pltpu.VMEM((heads, LANES), F32),
                pltpu.VMEM((count, heads, head), BF16),
                pltpu.VMEM((count, 1, LANES), F32),
                pltpu.VMEM((places, n, heads, head), BF16),
                pltpu.VMEM((places, n, 1, LANES), F32),
                dma((3, SLOTS)),
                dma((2, count)),
                dma((2, places, n)),
                dma((owned, n)),
                dma((count,)),
                dma((2, LAST, n)),
            ],
            compiler_params=pltpu.CompilerParams(collective_id=0, has_side_effects=True, vmem_limit_bytes=63 * 2**20),
        )(q, k.reshape(-1, head), v.reshape(-1, head))

    return jax.shard_map(
        step,
        mesh=mesh,
        in_specs=(P("dp", None, None), P("dp", "sp", None, None), P("dp", "sp", None, None)),
        out_specs=P("dp", None, None),
        check_vma=False,
    )
```

time: 269 us -> 88.9 us (0.33)
  waiting for transfers between devices: 148 us -> 0 us
  Pallas kernels: 0 us -> 86.9 us
  matrix products: 85 us -> 0 us
  other arithmetic: 19 us -> 0 us
  between operations: 13.4 us -> 0.01 us
    all_gather x1 -> x0, waiting for transfers between devices: 148 us -> none  [step(): return together(lax.all_gather(part_of(q, k, v), 'sp')).reshape(q.shape)]
    pallas_call x0 -> x1, Pallas kernels: none -> 86.9 us  [step(): pl.pallas_call(functools.partial(kernel, n, head ** (-0.5)), out_shape=ja...]
    dot_general x2 -> x0, matrix products: 85 us -> none  [einsum(): return jnp.einsum(form, a.astype(jnp.float32), b.astype(jnp.float32))]
    reduce_sum x2 -> x0, other arithmetic: 15.2 us -> none  [the longest x1 14.1 us: together(): jnp.sum(seen * scale, 0) / jnp.sum(total * scale, 0)]
  transfers between devices with their start and end apart: 1 -> 0, of which waited for: 1 -> 0; matrix products, arithmetic and copies ran while one was open for 0% -> 0% of each run, Pallas kernels for 0% -> 0%
where the time goes in v1:
time: 88.9 us; the launch traced here: 88.7 us
  Pallas kernels  86.9 us (98%)
  local copies, waits for them, and re-layouts  1.82 us (2%)
    pallas_call x1, Pallas kernels, step(): pl.pallas_call(functools.partial(kernel, n, head ** (-0.5)), out_shape=ja...  86.9 us
    unnamed x1, local copies, waits for them, and re-layouts  1.82 us

profile of v1, /device:TPU:0, one launch (start us, length us, event | category | flops | bytes accessed | tf_op | source)
XLA Modules:
  0.0 88.7 jit_solution(8429293615716589577)
XLA Ops:
  0.0 86.9 %shard_map.37 = bf16[32,56,128]{2,1,0:T(8,128)(2,1)} custom-call(bf16[32,56,128]{2,1,0:T(8,128)(2,1)} %q_hbm.1, bf16[458752,128]{1,0:T(8,128)(2,1)} %bitcast.k_hbm, bf16[458752,128]{1,0:T(8,128)(2,1)} %bitcast.1.v_hbm), custom_call_target="tpu_custom_call" | custom-call | tf_op jit(solution)/shard_map/pallas_call | solution.py:265
  86.9 1.8 %copy.5 = bf16[32,56,128]{2,1,0:T(8,128)(2,1)} copy(bf16[32,56,128]{2,1,0:T(8,128)(2,1)} %shard_map.37) | data formatting | bytes 917504

commit v2 on v1

v2 whole, which is shorter than its diff:
```python
import functools

import jax
import jax.numpy as jnp
from jax import lax
from jax.experimental import pallas as pl
from jax.experimental.pallas import tpu as pltpu
from jax.sharding import PartitionSpec as P

F32, BF16 = jnp.float32, jnp.bfloat16
LOG2E = 1.4426950408889634
CHUNK = 32
SLOTS = 4
LAST = 1
PIECES = 4
DELAY = 3
SENT = 6
LANES = 128


def kernel(n, scale, q_hbm, k_hbm, v_hbm, out, q, keys, values, mask, scores, high, part, stats, parts, allstats, in_sem, end_sem, to_sems, to_semr, res_sems, res_semr, all_sems):
    count, heads, head = out.shape
    rows = keys.shape[1]
    chunk = CHUNK * heads
    chunks = rows // chunk
    owned = pl.cdiv(count, n)
    early = count - LAST
    me = lax.axis_index("sp")

    def fetch(i, which):
        slot = lax.rem(i, SLOTS)
        cache, here = ((k_hbm, keys), (v_hbm, values))[which]
        return pltpu.make_async_copy(cache.at[pl.ds(i * rows, rows)], here.at[slot], in_sem.at[which, slot])

    def fetch_end(piece):
        size = rows // PIECES
        i = count - 1
        return pltpu.make_async_copy(
            v_hbm.at[pl.ds(i * rows + piece * size, size)],
            values.at[i % SLOTS, pl.ds(piece * size, size)],
            end_sem.at[piece],
        )

    q_copy = pltpu.make_async_copy(q_hbm, q, in_sem.at[2, 0])
    q_copy.start()
    fetch(0, 0).start()
    for i in range(1, SLOTS):
        fetch(i, 0).start()
        fetch(i - 1, 1).start()

    barrier = pltpu.get_barrier_semaphore()
    for step in range(1, n):
        pl.semaphore_signal(barrier, inc=1, device_id={"sp": lax.rem(me + step, n)})

    column = lax.broadcasted_iota(jnp.int32, (heads, chunk), 1).astype(F32)
    column = column - heads * jnp.floor((column + 0.5) * (1 / heads))
    row = lax.broadcasted_iota(jnp.int32, (heads, chunk), 0).astype(F32)
    mask[...] = jnp.where(column == row, jnp.inf, -jnp.inf)

    lane = lax.broadcasted_iota(jnp.int32, (heads, LANES), 1)
    line = lax.broadcasted_iota(jnp.int32, (heads, LANES), 0)
    own_lane = lane == line

    def score(i, place):
        slot = lax.rem(i, SLOTS)
        best = []

        def one(j):
            got = lax.dot_general(q[i], keys[slot, pl.ds(j * chunk, chunk), :], (((1,), (1,)), ((), ())), preferred_element_type=F32)
            got = jnp.minimum(got, mask[...])
            scores[place, :, pl.ds(j * chunk, chunk)] = got
            for g in range(chunk // LANES):
                piece = got[:, g * LANES : (g + 1) * LANES]
                best[:] = [jnp.maximum(best[0], piece) if best else piece]

        def end():
            high[place] = jnp.broadcast_to(jnp.max(best[0], -1, keepdims=True), (heads, LANES))

        return one, end

    def value(i, place):
        slot = lax.rem(i, SLOTS)
        top = high[place]
        total, seen = [], []

        def one(j):
            weights = []
            for g in range(chunk // LANES):
                w = jnp.exp2((scores[place, :, pl.ds(j * chunk + g * LANES, LANES)] - top) * (scale * LOG2E))
                total[:] = [total[0] + w if total else w]
                weights.append(w.astype(BF16))
            got = jnp.dot(jnp.concatenate(weights, 1), values[slot, pl.ds(j * chunk, chunk), :], preferred_element_type=F32)
            seen[:] = [seen[0] + got if seen else got]

        def end():
            sums = jnp.sum(total[0], -1, keepdims=True)
            part[i] = seen[0].astype(BF16)
            both = jnp.where(own_lane, top, 0.0) + jnp.where(lane == line + LANES // 2, sums, 0.0)
            stats[i] = jnp.sum(both, 0, keepdims=True)

        return one, end

    def part_copies(i, place, there, sems):
        return [
            pltpu.make_async_remote_copy(part.at[i], parts.at[place, me], sems[0], to_semr.at[0, place], device_id={"sp": there}),
            pltpu.make_async_remote_copy(stats.at[i], allstats.at[place, me], sems[1], to_semr.at[1, place], device_id={"sp": there}),
        ]

    def to_owner(i):
        return part_copies(i, i // n, lax.rem(i, n), (to_sems.at[0, i], to_sems.at[1, i]))

    def keep(i, place):
        parts[place, me] = part[i]
        allstats[place, me] = stats[i]

    def other(flips):
        there = me
        for bit in range(4):
            if flips >> bit & 1:
                there = there + (1 - 2 * lax.rem(me // 2**bit, 2)) * 2**bit
        return there

    order = sorted(range(1, n), key=lambda flips: (-bin(flips >> 1).count("1"), flips))

    def to_all(i):
        which = i - early
        for flips in order:
            for copy in part_copies(i, owned + which, other(flips), (all_sems.at[0, which], all_sems.at[1, which])):
                copy.start()
        keep(i, owned + which)

    def all_bytes(sem_part, sem_stats):
        for ref, sem in ((parts, sem_part), (allstats, sem_stats)):
            ref = ref.at[0, pl.ds(0, n - 1)]
            pltpu.make_async_copy(ref, ref, sem).wait()

    def combine(place, i):
        all_bytes(to_semr.at[0, place], to_semr.at[1, place])
        both = jnp.concatenate([allstats[place, s] for s in range(n)], 0)
        sums = pltpu.roll(both, LANES // 2, 1)
        share = jnp.exp2((both - jnp.max(both, 0, keepdims=True)) * (scale * LOG2E))
        share = share / jnp.sum(share * sums, 0, keepdims=True)
        got = None
        for s in range(n):
            mine = jnp.broadcast_to(share[s : s + 1], (heads, LANES))
            mine = jnp.sum(jnp.where(own_lane, mine, 0.0), -1, keepdims=True)
            term = mine * parts[place, s].astype(F32)
            got = term if got is None else got + term
        out[i] = got.astype(BF16)

    def finish(i):
        @pl.when(lax.rem(i, n) == me)
        def _():
            place = i // n
            combine(place, i)
            for flips in order:
                pltpu.make_async_remote_copy(out.at[i], out.at[i], res_sems.at[place], res_semr.at[0], device_id={"sp": other(flips)}).start()

    def sent(i):
        @pl.when(lax.rem(i, n) != me)
        def _():
            for copy in to_owner(i):
                copy.wait_send()

    q_copy.wait()
    fetch(0, 0).wait()
    one, end = score(0, 0)
    for j in range(chunks):
        one(j)
    end()
    pl.semaphore_wait(barrier, n - 1)

    def step(i, _):
        @pl.when(i < count - 5)
        def _():
            fetch(i + SLOTS - 2, 1).start()
            fetch(i + SLOTS - 1, 0).start()

        @pl.when(i == count - 5)
        def _():
            fetch(count - 2, 0).start()

        @pl.when(i == count - 4)
        def _():
            fetch(count - 1, 0).start()
            fetch(count - 3, 1).start()
            fetch(count - 2, 1).start()

        @pl.when(i == count - 3)
        def _():
            for piece in range(PIECES):
                fetch_end(piece).start()

        fetch(i, 0).wait()
        fetch(i - 1, 1).wait()
        value_one, value_end = value(i - 1, 0)
        score_one, score_end = score(i, 0)
        for j in range(chunks):
            value_one(j)
            score_one(j)
        value_end()
        score_end()

        last = i - 1

        @pl.when(lax.rem(last, n) != me)
        def _():
            for copy in to_owner(last):
                copy.start()

        @pl.when(lax.rem(last, n) == me)
        def _():
            keep(last, last // n)

        @pl.when(last >= DELAY)
        def _():
            finish(last - DELAY)

        @pl.when(last >= SENT)
        def _():
            sent(last - SENT)

        return 0

    lax.fori_loop(1, count - 2, step, 0)

    for place, i in enumerate((count - 2, count - 1), 1):
        fetch(i, 0).wait()
        one, end = score(i, place)
        for j in range(chunks):
            one(j)
        end()
        if count - 3 - DELAY + place - 1 < early - 1:
            finish(count - 3 - DELAY + place - 1)

    for place, i in enumerate((count - 3, count - 2, count - 1)):
        pieces = PIECES if i == count - 1 else 1
        one, end = value(i, place)
        for piece in range(pieces):
            if i == count - 1:
                fetch_end(piece).wait()
            else:
                fetch(i, 1).wait()
            for j in range(piece * chunks // pieces, (piece + 1) * chunks // pieces):
                one(j)
        end()
        if i < early:
            @pl.when(lax.rem(i, n) != me)
            def _():
                for copy in to_owner(i):
                    copy.start()

            @pl.when(lax.rem(i, n) == me)
            def _():
                keep(i, i // n)
        else:
            to_all(i)

    for i in range(count - 3 - DELAY + 2, early):
        finish(i)
    for i in range(early, count):
        combine(owned + i - early, i)

    for i in range(count - 3 - SENT, early):
        sent(i)
    most = pl.cdiv(early, n)
    for mine in (most - 1, most):
        @pl.when((early + n - 1 - me) // n == mine)
        def _():
            ref = out.at[pl.ds(0, early - mine)]
            pltpu.make_async_copy(ref, ref, res_semr.at[0]).wait()
            ref = out.at[pl.ds(0, n - 1)]
            for place in range(mine):
                pltpu.make_async_copy(ref, ref, res_sems.at[place]).wait()

    for which in range(LAST):
        all_bytes(all_sems.at[0, which], all_sems.at[1, which])


def solution(mesh):
    n = mesh.shape["sp"]

    def step(q, k, v):
        count, tokens, heads, head = k.shape
        rows = tokens * heads
        owned = pl.cdiv(count, n)
        places = owned + LAST
        anywhere = pl.BlockSpec(memory_space=pl.ANY)
        dma = pltpu.SemaphoreType.DMA
        return pl.pallas_call(
            functools.partial(kernel, n, head**-0.5),
            out_shape=jax.ShapeDtypeStruct(q.shape, BF16),
            in_specs=[pl.BlockSpec(memory_space=pltpu.HBM), anywhere, anywhere],
            out_specs=pl.BlockSpec(memory_space=pltpu.VMEM),
            scratch_shapes=[
                pltpu.VMEM(q.shape, BF16),
                pltpu.VMEM((SLOTS, rows, head), BF16),
                pltpu.VMEM((SLOTS, rows, head), BF16),
                pltpu.VMEM((heads, CHUNK * heads), F32),
                pltpu.VMEM((3, heads, rows), F32),
                pltpu.VMEM((3, heads, LANES), F32),
                pltpu.VMEM((count, heads, head), BF16),
                pltpu.VMEM((count, 1, LANES), F32),
                pltpu.VMEM((places, n, heads, head), BF16),
                pltpu.VMEM((places, n, 1, LANES), F32),
                dma((3, SLOTS)),
                dma((PIECES,)),
                dma((2, count)),
                dma((2, places)),
                dma((owned,)),
                dma((1,)),
                dma((2, LAST)),
            ],
            compiler_params=pltpu.CompilerParams(collective_id=0, has_side_effects=True, vmem_limit_bytes=48 * 2**20),
        )(pltpu.with_memory_space_constraint(q, pltpu.HBM), k.reshape(-1, head), v.reshape(-1, head))

    return jax.shard_map(
        step,
        mesh=mesh,
        in_specs=(P("dp", None, None), P("dp", "sp", None, None), P("dp", "sp", None, None)),
        out_specs=P("dp", None, None),
        check_vma=False,
    )
```

time: 88.9 us -> 83 us (0.934)
  Pallas kernels: 86.9 us -> 82.1 us
  local copies, waits for them, and re-layouts: 1.82 us -> 0.77 us
    pallas_call x1, Pallas kernels: 86.9 us -> 82.1 us  [step(): pl.pallas_call(functools.partial(kernel, n, head ** (-0.5)), out_shape=ja...]
    unnamed x1, local copies, waits for them, and re-layouts: 1.82 us -> 0.77 us
where the time goes in v2:
time: 83 us; the launch traced here: 82.9 us
  Pallas kernels  82.1 us (99%)
    pallas_call x1, Pallas kernels, step(): pl.pallas_call(functools.partial(kernel, n, head ** (-0.5)), out_shape=ja...  82.1 us

profile of v2, /device:TPU:0, one launch (start us, length us, event | category | flops | bytes accessed | tf_op | source)
XLA Modules:
  0.0 82.9 jit_solution(3535327852296803978)
XLA Ops:
  0.0 82.1 %shard_map.37 = bf16[32,56,128]{2,1,0:T(8,128)(2,1)S(1)} custom-call(bf16[32,56,128]{2,1,0:T(8,128)(2,1)} %q_hbm.1, bf16[458752,128]{1,0:T(8,128)(2,1)} %bitcast.k_hbm, bf16[458752,128]{1,0:T(8,128)(2,1)} %bitcast.1.v_hbm), custom_call_target="tpu_custom_call" | custom-call | tf_op jit(solution)/shard_map/pallas_call | solution.py:290
  82.1 0.8 copy.5

commit v3 on v2

--- a/solution.py
+++ b/solution.py
@@ -11,14 +11,14 @@
 LOG2E = 1.4426950408889634
 CHUNK = 32
 SLOTS = 4
-LAST = 1
+LAST = 3
 PIECES = 4
 DELAY = 3
 SENT = 6
 LANES = 128
 
 
-def kernel(n, scale, q_hbm, k_hbm, v_hbm, out, q, keys, values, mask, scores, high, part, stats, parts, allstats, in_sem, end_sem, to_sems, to_semr, res_sems, res_semr, all_sems):
+def kernel(n, scale, q_hbm, k_hbm, v_hbm, out, q, keys, values, mask, scores, high, part, stats, parts, allstats, in_sem, end_sem, to_sems, to_semr, res_sems, res_semr, mine, halves, pair, pairstats, both, bothstats, alls, allsstats, pair_sems, pair_semr, all_sems, all_semr):
     count, heads, head = out.shape
     rows = keys.shape[1]
     chunk = CHUNK * heads
@@ -94,9 +94,9 @@
 
         def end():
             sums = jnp.sum(total[0], -1, keepdims=True)
-            part[i] = seen[0].astype(BF16)
-            both = jnp.where(own_lane, top, 0.0) + jnp.where(lane == line + LANES // 2, sums, 0.0)
-            stats[i] = jnp.sum(both, 0, keepdims=True)
+            known = jnp.where(own_lane, top, 0.0) + jnp.where(lane == line + LANES // 2, sums, 0.0)
+            stats[i] = jnp.sum(known, 0, keepdims=True)
+            return seen[0]
 
         return one, end
 
@@ -122,29 +122,87 @@
 
     order = sorted(range(1, n), key=lambda flips: (-bin(flips >> 1).count("1"), flips))
 
+    core = lax.rem(me, 2)
+    half = halves.shape[2]
+    cuts = (0, heads - half)
+    line_half = lax.broadcasted_iota(jnp.int32, (half, LANES), 0)
+    lane_half = lax.broadcasted_iota(jnp.int32, (half, LANES), 1)
+    low = lax.broadcasted_iota(jnp.int32, (1, LANES), 1) < LANES // 2
+
+    def swap(which, i):
+        there = other(1)
+        return [
+            pltpu.make_async_remote_copy(halves.at[which, 1 - core], pair.at[which], pair_sems.at[0, which], pair_semr.at[0, which], device_id={"sp": there}),
+            pltpu.make_async_remote_copy(stats.at[i], pairstats.at[which], pair_sems.at[1, which], pair_semr.at[1, which], device_id={"sp": there}),
+        ]
+
+    def to_pair(i, seen):
+        which = i - early
+        for c, cut in enumerate(cuts):
+            mine[which, c] = seen[cut : cut + half]
+            halves[which, c] = seen[cut : cut + half].astype(BF16)
+        for copy in swap(which, i):
+            copy.start()
+
+    def all_copies(which, there):
+        return [
+            pltpu.make_async_remote_copy(both.at[which], alls.at[which, me], all_sems.at[0, which], all_semr.at[0, which], device_id={"sp": there}),
+            pltpu.make_async_remote_copy(bothstats.at[which], allsstats.at[which, me], all_sems.at[1, which], all_semr.at[1, which], device_id={"sp": there}),
+        ]
+
     def to_all(i):
         which = i - early
+        for copy in swap(which, i):
+            copy.wait_recv()
+        a, b = stats[i], pairstats[which]
+        top = jnp.maximum(a, b)
+        a_share, b_share = jnp.exp2((a - top) * (scale * LOG2E)), jnp.exp2((b - top) * (scale * LOG2E))
+        sums = a_share * pltpu.roll(a, LANES // 2, 1) + b_share * pltpu.roll(b, LANES // 2, 1)
+        known = jnp.where(low, top, pltpu.roll(sums, LANES // 2, 1))
+        own = lane_half == line_half + core * cuts[1]
+        a_share, b_share = (jnp.sum(jnp.where(own, jnp.broadcast_to(x, own.shape), 0.0), -1, keepdims=True) for x in (a_share, b_share))
+        got = (a_share * mine[which, core] + b_share * pair[which].astype(F32)).astype(BF16)
+        both[which] = got
+        bothstats[which] = known
         for flips in order:
-            for copy in part_copies(i, owned + which, other(flips), (all_sems.at[0, which], all_sems.at[1, which])):
+            for copy in all_copies(which, other(flips)):
                 copy.start()
-        keep(i, owned + which)
-
-    def all_bytes(sem_part, sem_stats):
-        for ref, sem in ((parts, sem_part), (allstats, sem_stats)):
-            ref = ref.at[0, pl.ds(0, n - 1)]
-            pltpu.make_async_copy(ref, ref, sem).wait()
+        alls[which, me] = got
+        allsstats[which, me] = known
+
+    def combine_all(i):
+        which = i - early
+        some_bytes(alls, all_semr.at[0, which])
+        some_bytes(allsstats, all_semr.at[1, which])
+        done = []
+        for c, cut in enumerate(cuts):
+            share = shares(jnp.concatenate([allsstats[which, s] for s in range(c, n, 2)], 0))
+            start = half - cut if c else 0
+            own = own_lane[cut + start : cut + half]
+            got = None
+            for j, s in enumerate(range(c, n, 2)):
+                column = jnp.sum(jnp.where(own, jnp.broadcast_to(share[j : j + 1], own.shape), 0.0), -1, keepdims=True)
+                term = column * alls[which, s].astype(F32)[start:]
+                got = term if got is None else got + term
+            done.append(got)
+        out[i] = jnp.concatenate(done, 0).astype(BF16)
+
+    def some_bytes(ref, sem):
+        ref = ref.at[0, pl.ds(0, n - 1)]
+        pltpu.make_async_copy(ref, ref, sem).wait()
+
+    def shares(known):
+        share = jnp.exp2((known - jnp.max(known, 0, keepdims=True)) * (scale * LOG2E))
+        return share / jnp.sum(share * pltpu.roll(known, LANES // 2, 1), 0, keepdims=True)
 
     def combine(place, i):
-        all_bytes(to_semr.at[0, place], to_semr.at[1, place])
-        both = jnp.concatenate([allstats[place, s] for s in range(n)], 0)
-        sums = pltpu.roll(both, LANES // 2, 1)
-        share = jnp.exp2((both - jnp.max(both, 0, keepdims=True)) * (scale * LOG2E))
-        share = share / jnp.sum(share * sums, 0, keepdims=True)
+        some_bytes(parts, to_semr.at[0, place])
+        some_bytes(allstats, to_semr.at[1, place])
+        share = shares(jnp.concatenate([allstats[place, s] for s in range(n)], 0))
         got = None
         for s in range(n):
-            mine = jnp.broadcast_to(share[s : s + 1], (heads, LANES))
-            mine = jnp.sum(jnp.where(own_lane, mine, 0.0), -1, keepdims=True)
-            term = mine * parts[place, s].astype(F32)
+            column = jnp.sum(jnp.where(own_lane, jnp.broadcast_to(share[s : s + 1], (heads, LANES)), 0.0), -1, keepdims=True)
+            term = column * parts[place, s].astype(F32)
             got = term if got is None else got + term
         out[i] = got.astype(BF16)
 
@@ -198,10 +256,9 @@
         for j in range(chunks):
             value_one(j)
             score_one(j)
-        value_end()
+        last = i - 1
+        part[last] = value_end().astype(BF16)
         score_end()
-
-        last = i - 1
 
         @pl.when(lax.rem(last, n) != me)
         def _():
@@ -243,38 +300,33 @@
                 fetch(i, 1).wait()
             for j in range(piece * chunks // pieces, (piece + 1) * chunks // pieces):
                 one(j)
-        end()
-        if i < early:
-            @pl.when(lax.rem(i, n) != me)
-            def _():
-                for copy in to_owner(i):
-                    copy.start()
-
-            @pl.when(lax.rem(i, n) == me)
-            def _():
-                keep(i, i // n)
-        else:
-            to_all(i)
-
+        to_pair(i, end())
+        if i > early:
+            to_all(i - 1)
     for i in range(count - 3 - DELAY + 2, early):
         finish(i)
+    to_all(count - 1)
     for i in range(early, count):
-        combine(owned + i - early, i)
+        combine_all(i)
 
     for i in range(count - 3 - SENT, early):
         sent(i)
     most = pl.cdiv(early, n)
-    for mine in (most - 1, most):
-        @pl.when((early + n - 1 - me) // n == mine)
-        def _():
-            ref = out.at[pl.ds(0, early - mine)]
+    for number in (most - 1, most):
+
+        @pl.when((early + n - 1 - me) // n == number)
+        def _():
+            ref = out.at[pl.ds(0, early - number)]
             pltpu.make_async_copy(ref, ref, res_semr.at[0]).wait()
             ref = out.at[pl.ds(0, n - 1)]
-            for place in range(mine):
+            for place in range(number):
                 pltpu.make_async_copy(ref, ref, res_sems.at[place]).wait()
 
     for which in range(LAST):
-        all_bytes(all_sems.at[0, which], all_sems.at[1, which])
+        for copy in swap(which, early + which):
+            copy.wait_send()
+        some_bytes(alls, all_sems.at[0, which])
+        some_bytes(allsstats, all_sems.at[1, which])
 
 
 def solution(mesh):
@@ -284,7 +336,7 @@
         count, tokens, heads, head = k.shape
         rows = tokens * heads
         owned = pl.cdiv(count, n)
-        places = owned + LAST
+        half = heads * 4 // 7
         anywhere = pl.BlockSpec(memory_space=pl.ANY)
         dma = pltpu.SemaphoreType.DMA
         return pl.pallas_call(
@@ -301,14 +353,25 @@
                 pltpu.VMEM((3, heads, LANES), F32),
                 pltpu.VMEM((count, heads, head), BF16),
                 pltpu.VMEM((count, 1, LANES), F32),
-                pltpu.VMEM((places, n, heads, head), BF16),
-                pltpu.VMEM((places, n, 1, LANES), F32),
+                pltpu.VMEM((owned, n, heads, head), BF16),
+                pltpu.VMEM((owned, n, 1, LANES), F32),
                 dma((3, SLOTS)),
                 dma((PIECES,)),
                 dma((2, count)),
-                dma((2, places)),
+                dma((2, owned)),
                 dma((owned,)),
                 dma((1,)),
+                pltpu.VMEM((LAST, 2, half, head), F32),
+                pltpu.VMEM((LAST, 2, half, head), BF16),
+                pltpu.VMEM((LAST, half, head), BF16),
+                pltpu.VMEM((LAST, 1, LANES), F32),
+                pltpu.VMEM((LAST, half, head), BF16),
+                pltpu.VMEM((LAST, 1, LANES), F32),
+                pltpu.VMEM((LAST, n, half, head), BF16),
+                pltpu.VMEM((LAST, n, 1, LANES), F32),
+                dma((2, LAST)),
+                dma((2, LAST)),
+                dma((2, LAST)),
                 dma((2, LAST)),
             ],
             compiler_params=pltpu.CompilerParams(collective_id=0, has_side_effects=True, vmem_limit_bytes=48 * 2**20),

time: 83 us -> 83.9 us (1.011)
  Pallas kernels: 82.1 us -> 83 us
    pallas_call x1, Pallas kernels: 82.1 us -> 83 us  [step(): pl.pallas_call(functools.partial(kernel, n, head ** (-0.5)), out_shape=ja...]
where the time goes in v3:
time: 83.9 us; the launch traced here: 83.8 us
  Pallas kernels  83 us (99%)
    pallas_call x1, Pallas kernels, step(): pl.pallas_call(functools.partial(kernel, n, head ** (-0.5)), out_shape=ja...  83 us

profile of v3, /device:TPU:0, one launch (start us, length us, event | category | flops | bytes accessed | tf_op | source)
XLA Modules:
  0.0 83.8 jit_solution(10774008231566206436)
XLA Ops:
  0.0 83.0 %shard_map.37 = bf16[32,56,128]{2,1,0:T(8,128)(2,1)S(1)} custom-call(bf16[32,56,128]{2,1,0:T(8,128)(2,1)} %q_hbm.1, bf16[458752,128]{1,0:T(8,128)(2,1)} %bitcast.k_hbm, bf16[458752,128]{1,0:T(8,128)(2,1)} %bitcast.1.v_hbm), custom_call_target="tpu_custom_call" | custom-call | tf_op jit(solution)/shard_map/pallas_call | solution.py:342
  83.0 0.8 copy.5

commit v4 on v3

--- a/solution.py
+++ b/solution.py
@@ -12,13 +12,12 @@
 CHUNK = 32
 SLOTS = 4
 LAST = 3
-PIECES = 4
 DELAY = 3
-SENT = 6
+SENT = 3
 LANES = 128
 
 
-def kernel(n, scale, q_hbm, k_hbm, v_hbm, out, q, keys, values, mask, scores, high, part, stats, parts, allstats, in_sem, end_sem, to_sems, to_semr, res_sems, res_semr, mine, halves, pair, pairstats, both, bothstats, alls, allsstats, pair_sems, pair_semr, all_sems, all_semr):
+def kernel(n, scale, q_hbm, k_hbm, v_hbm, out, q, keys, values, mask, scores, high, part, stats, parts, allstats, in_sem, to_sems, to_semr, res_sems, res_semr, mine, halves, pair, pairstats, both, bothstats, alls, allsstats, pair_sems, pair_semr, all_sems, all_semr):
     count, heads, head = out.shape
     rows = keys.shape[1]
     chunk = CHUNK * heads
@@ -31,15 +30,6 @@
         slot = lax.rem(i, SLOTS)
         cache, here = ((k_hbm, keys), (v_hbm, values))[which]
         return pltpu.make_async_copy(cache.at[pl.ds(i * rows, rows)], here.at[slot], in_sem.at[which, slot])
-
-    def fetch_end(piece):
-        size = rows // PIECES
-        i = count - 1
-        return pltpu.make_async_copy(
-            v_hbm.at[pl.ds(i * rows + piece * size, size)],
-            values.at[i % SLOTS, pl.ds(piece * size, size)],
-            end_sem.at[piece],
-        )
 
     q_copy = pltpu.make_async_copy(q_hbm, q, in_sem.at[2, 0])
     q_copy.start()
@@ -106,8 +96,11 @@
             pltpu.make_async_remote_copy(stats.at[i], allstats.at[place, me], sems[1], to_semr.at[1, place], device_id={"sp": there}),
         ]
 
+    def owner(i):
+        return lax.rem(i, n // 2) * 2 + lax.rem(i // (n // 2), 2)
+
     def to_owner(i):
-        return part_copies(i, i // n, lax.rem(i, n), (to_sems.at[0, i], to_sems.at[1, i]))
+        return part_copies(i, i // n, owner(i), (to_sems.at[0, lax.rem(i, SENT + 1)], to_sems.at[1, lax.rem(i, SENT + 1)]))
 
     def keep(i, place):
         parts[place, me] = part[i]
@@ -207,15 +200,25 @@
         out[i] = got.astype(BF16)
 
     def finish(i):
-        @pl.when(lax.rem(i, n) == me)
+        @pl.when(owner(i) == me)
         def _():
             place = i // n
             combine(place, i)
             for flips in order:
                 pltpu.make_async_remote_copy(out.at[i], out.at[i], res_sems.at[place], res_semr.at[0], device_id={"sp": other(flips)}).start()
 
+    def send(i):
+        @pl.when(owner(i) != me)
+        def _():
+            for copy in to_owner(i):
+                copy.start()
+
+        @pl.when(owner(i) == me)
+        def _():
+            keep(i, i // n)
+
     def sent(i):
-        @pl.when(lax.rem(i, n) != me)
+        @pl.when(owner(i) != me)
         def _():
             for copy in to_owner(i):
                 copy.wait_send()
@@ -229,25 +232,11 @@
     pl.semaphore_wait(barrier, n - 1)
 
     def step(i, _):
-        @pl.when(i < count - 5)
-        def _():
-            fetch(i + SLOTS - 2, 1).start()
+        fetch(i + SLOTS - 2, 1).start()
+
+        @pl.when(i + SLOTS - 1 < count)
+        def _():
             fetch(i + SLOTS - 1, 0).start()
-
-        @pl.when(i == count - 5)
-        def _():
-            fetch(count - 2, 0).start()
-
-        @pl.when(i == count - 4)
-        def _():
-            fetch(count - 1, 0).start()
-            fetch(count - 3, 1).start()
-            fetch(count - 2, 1).start()
-
-        @pl.when(i == count - 3)
-        def _():
-            for piece in range(PIECES):
-                fetch_end(piece).start()
 
         fetch(i, 0).wait()
         fetch(i - 1, 1).wait()
@@ -260,14 +249,7 @@
         part[last] = value_end().astype(BF16)
         score_end()
 
-        @pl.when(lax.rem(last, n) != me)
-        def _():
-            for copy in to_owner(last):
-                copy.start()
-
-        @pl.when(lax.rem(last, n) == me)
-        def _():
-            keep(last, last // n)
+        send(last)
 
         @pl.when(last >= DELAY)
         def _():
@@ -281,40 +263,41 @@
 
     lax.fori_loop(1, count - 2, step, 0)
 
-    for place, i in enumerate((count - 2, count - 1), 1):
+    def score_alone(i, place):
         fetch(i, 0).wait()
         one, end = score(i, place)
         for j in range(chunks):
             one(j)
         end()
-        if count - 3 - DELAY + place - 1 < early - 1:
-            finish(count - 3 - DELAY + place - 1)
-
-    for place, i in enumerate((count - 3, count - 2, count - 1)):
-        pieces = PIECES if i == count - 1 else 1
+
+    def value_alone(i, place):
+        fetch(i, 1).wait()
         one, end = value(i, place)
-        for piece in range(pieces):
-            if i == count - 1:
-                fetch_end(piece).wait()
-            else:
-                fetch(i, 1).wait()
-            for j in range(piece * chunks // pieces, (piece + 1) * chunks // pieces):
-                one(j)
-        to_pair(i, end())
-        if i > early:
-            to_all(i - 1)
-    for i in range(count - 3 - DELAY + 2, early):
-        finish(i)
-    to_all(count - 1)
+        for j in range(chunks):
+            one(j)
+        return end()
+
+    a, b, c = range(early, count)
+    score_alone(b, 1)
+    finish(early - 3)
+    to_pair(a, value_alone(a, 0))
+    score_alone(c, 0)
+    to_all(a)
+    finish(early - 2)
+    to_pair(b, value_alone(b, 1))
+    finish(early - 1)
+    to_pair(c, value_alone(c, 0))
+    to_all(b)
+    to_all(c)
     for i in range(early, count):
         combine_all(i)
 
-    for i in range(count - 3 - SENT, early):
+    for i in range(early - SENT, early):
         sent(i)
     most = pl.cdiv(early, n)
     for number in (most - 1, most):
 
-        @pl.when((early + n - 1 - me) // n == number)
+        @pl.when((early + n - 1 - me // 2 - lax.rem(me, 2) * (n // 2)) // n == number)
         def _():
             ref = out.at[pl.ds(0, early - number)]
             pltpu.make_async_copy(ref, ref, res_semr.at[0]).wait()
@@ -349,15 +332,14 @@
                 pltpu.VMEM((SLOTS, rows, head), BF16),
                 pltpu.VMEM((SLOTS, rows, head), BF16),
                 pltpu.VMEM((heads, CHUNK * heads), F32),
-                pltpu.VMEM((3, heads, rows), F32),
-                pltpu.VMEM((3, heads, LANES), F32),
+                pltpu.VMEM((2, heads, rows), F32),
+                pltpu.VMEM((2, heads, LANES), F32),
                 pltpu.VMEM((count, heads, head), BF16),
                 pltpu.VMEM((count, 1, LANES), F32),
                 pltpu.VMEM((owned, n, heads, head), BF16),
                 pltpu.VMEM((owned, n, 1, LANES), F32),
                 dma((3, SLOTS)),
-                dma((PIECES,)),
-                dma((2, count)),
+                dma((2, SENT + 1)),
                 dma((2, owned)),
                 dma((owned,)),
                 dma((1,)),

time: 83.9 us -> 82 us (0.977)
  Pallas kernels: 83 us -> 81.1 us
    pallas_call x1, Pallas kernels: 83 us -> 81.1 us  [step(): pl.pallas_call(functools.partial(kernel, n, head ** (-0.5)), out_shape=ja...]
where the time goes in v4:
time: 82 us; the launch traced here: 81.8 us
  Pallas kernels  81.1 us (99%)
    pallas_call x1, Pallas kernels, step(): pl.pallas_call(functools.partial(kernel, n, head ** (-0.5)), out_shape=ja...  81.1 us

profile of v4, /device:TPU:0, one launch (start us, length us, event | category | flops | bytes accessed | tf_op | source)
XLA Modules:
  0.0 81.8 jit_solution(9841067362737549816)
XLA Ops:
  0.0 81.1 %shard_map.37 = bf16[32,56,128]{2,1,0:T(8,128)(2,1)S(1)} custom-call(bf16[32,56,128]{2,1,0:T(8,128)(2,1)} %q_hbm.1, bf16[458752,128]{1,0:T(8,128)(2,1)} %bitcast.k_hbm, bf16[458752,128]{1,0:T(8,128)(2,1)} %bitcast.1.v_hbm), custom_call_target="tpu_custom_call" | custom-call | tf_op jit(solution)/shard_map/pallas_call | solution.py:325
  81.1 0.8 copy.5
